TPU v7x, 32 devices: a whole 2x2x4 slice. The times are simulated.
32 devices in a mesh: slab: 16 (over z, y, x), feat: 2 (over core).
Axes of the slice: x: 2, y: 2, z: 4, core: 2. Of those that a mesh axis runs over, the one named last changes fastest.
Arguments:
- states: float32 [40, 8192], P(None, ('slab', 'feat')), may hold values from -6 to 6
- inputs: float32 [8192], P(('slab', 'feat')), may hold values from -4 to 4
- targets: float32 [40, 8192], P(None, ('slab', 'feat')), may hold values from -4 to 4
Outputs:
- local_operators: float32 [16, 40, 862], P('slab', 'feat')
- scaled_duals: float32 [16, 40, 862], P('slab', 'feat')
- consensus: float32 [40, 862], P('feat')
- residual_history: float32 [2, 2], replicated
All inputs are finite; a program needn't handle non-finite values.
Results may differ from a plain program's by a relative error of at most 0.0003.
Values sent between devices are 32-bit elements; how exact they have to be, the bound alone decides.
No kernel may reach another device: no remote copies, remote signals or barrier semaphores. Data moves between devices by JAX's collectives and lax.ppermute only.
A program may use at most 64 MiB of HBM per device.

v0:
```python
import jax
import jax.numpy as jnp
from jax import lax
from jax.sharding import PartitionSpec as P

ITERS = 2
penalty = 1.0


def features(states, inputs):
    reduced = states.shape[0]
    blocks = [states]
    for column in range(reduced):
        blocks.append(states[column : column + 1] * states[column:])
    blocks.append(inputs[None, :])
    blocks.append(jnp.ones_like(inputs)[None, :])
    return jnp.concatenate(blocks, 0)


def product(left, right):
    return jnp.dot(left, right, precision=lax.Precision.HIGHEST, preferred_element_type=jnp.float32)


def solve_rows(factor, right_side):
    return jax.scipy.linalg.cho_solve((factor, True), right_side.T).T


def slab_average(summand):
    return lax.psum(summand, "slab")


def shards(states, inputs, targets):
    reduced = states.shape[0]
    feat_count = lax.axis_size("feat")
    slab_count = lax.axis_size("slab")
    half_rows = reduced // feat_count
    all_states, all_targets, all_inputs = (
        lax.all_gather(states, "feat", axis=1, tiled=True),
        lax.all_gather(targets, "feat", axis=1, tiled=True),
        lax.all_gather(inputs, "feat", axis=0, tiled=True),
    )
    design = features(all_states, all_inputs)
    row_total = design.shape[1]
    gram_matrix = product(design, design.T) / row_total
    first_row = lax.axis_index("feat") * half_rows
    picked = lax.dynamic_slice_in_dim(all_targets, first_row, half_rows, 0)
    cross = product(picked, design.T) / row_total
    width = gram_matrix.shape[0]
    factor = jnp.linalg.cholesky(gram_matrix + penalty * jnp.eye(width, dtype=jnp.float32))
    consensus = jnp.zeros((half_rows, width), jnp.float32)
    duals = jnp.zeros((half_rows, width), jnp.float32)
    operator_rows = duals
    primal_list = []
    dual_list = []
    for sweep in range(ITERS):
        operator_rows = solve_rows(factor, cross + penalty * (consensus - duals))
        updated = slab_average(operator_rows + duals) / slab_count
        duals = duals + operator_rows - updated
        primal_part = jnp.sum(jnp.square(operator_rows - updated))
        dual_part = penalty * penalty * jnp.sum(jnp.square(updated - consensus))
        primal_sum, dual_sum = lax.psum((primal_part, dual_part), ("slab", "feat"))
        primal_list.append(primal_sum)
        dual_list.append(dual_sum)
        consensus = updated
    history = jnp.stack([jnp.stack(primal_list), jnp.stack(dual_list)])
    residual_history = jnp.sqrt(history / (slab_count * reduced * width))
    return (operator_rows[None], duals[None], consensus, residual_history)


def solution(mesh):
    in_specs = (P(None, ("slab", "feat")), P(("slab", "feat")), P(None, ("slab", "feat")))
    out_specs = (P("slab", "feat", None), P("slab", "feat", None), P("feat", None), P())
    return jax.shard_map(shards, mesh=mesh, in_specs=in_specs, out_specs=out_specs, check_vma=False)
```

profile of v0, /device:TPU:0, one launch (start us, length us, event | category | flops | bytes accessed | tf_op | source)
XLA Modules:
  0.0 593.1 jit_solution(18076487294671778881)
XLA Ops:
  7.2 2.2 all_gather.9
  9.5 0.6 slice_multiply_fusion.38
  11.7 0.6 slice_multiply_fusion.26
  12.3 0.6 slice_multiply_fusion.25
  18.4 1.9 all-gather
  20.3 2.0 all_gather.11
  22.9 11.9 %concatenate.45 = f32[862,512]{1,0:T(8,128)S(1)} concatenate(f32[40,512]{1,0:T(8,128)S(1)} %all_gather.9, f32[40,512]{1,0:T(8,128)S(1)} %broadcast_multiply_fusion.1, f32[39,512]{1,0:T(8,128)S(1)} %slice_multiply_fusion.6, f32[38,512]{1,0:T(8,128)S(1)} %slice_multiply_fusion.5, f32[37,512]{1,0:T(8,128)S(1)} %slice_multiply_fusion.4, f32[36,512]{1,0:T(8,128)S(1)} %slice_multiply_fusion.3, ...), dimensions={0} | concatenate | bytes 3530752 | tf_op jit(solution)/shard_map/concatenate | solution.py:17
  34.8 7.8 %convert_add_fusion = (f32[862,862]{0,1:T(8,128)}, f32[862,862]{0,1:T(8,128)}) fusion(f32[862,512]{1,0:T(8,128)S(1)} %concatenate.45), kind=kOutput, calls=%fused_computation.8 | convolution fusion | flops 4568234496 | bytes 7709728 | tf_op jit(solution)/shard_map/dot_general | solution.py:21
  42.6 3.6 copy.12
  46.3 2.3 fusion.1
  48.5 1.6 copy-done.3
  50.2 11.7 %cholesky.196 = f32[128,128]{1,0:T(8,128)S(1)} custom-call(f32[128,128]{1,0:T(8,128)S(1)} %cholesky.508), custom_call_target="Cholesky" | custom-call | tf_op jit(solution)/shard_map/jit(cholesky)/cholesky | solution.py:49
  62.1 9.8 %custom-call.56 = f32[1,128,128]{1,2,0:T(8,128)S(1)} custom-call(f32[1,128,128]{2,1,0:T(8,128)S(1)} %get-tuple-element.104), custom_call_target="InvertDiagBlocksLowerTriangular" | custom-call | tf_op jit(solution)/shard_map/jit(cholesky)/cholesky | solution.py:49
  72.0 1.4 constant_dynamic-update-slice_fusion.62
  73.4 1.5 convolution_subtract_fusion
  74.9 0.6 cholesky.512
  75.5 12.5 %cholesky.217 = f32[128,128]{1,0:T(8,128)S(1)} custom-call(f32[128,128]{1,0:T(8,128)} %cholesky.512), custom_call_target="Cholesky" | custom-call | tf_op jit(solution)/shard_map/jit(cholesky)/cholesky | solution.py:49
  88.1 0.6 select_reduce_fusion.4
  88.7 11.0 %custom-call.57 = f32[1,128,128]{1,2,0:T(8,128)S(1)} custom-call(f32[1,128,128]{2,1,0:T(8,128)} %get-tuple-element.101), custom_call_target="InvertDiagBlocksLowerTriangular" | custom-call | tf_op jit(solution)/shard_map/jit(cholesky)/cholesky | solution.py:49
  100.1 1.6 convolution_subtract_fusion.1
  101.8 11.7 %cholesky.413 = f32[128,128]{1,0:T(8,128)S(1)} custom-call(f32[128,128]{1,0:T(8,128)S(1)} %cholesky.517), custom_call_target="Cholesky" | custom-call | tf_op jit(solution)/shard_map/jit(cholesky)/cholesky | solution.py:49
  113.5 9.8 %custom-call.58 = f32[1,128,128]{1,2,0:T(8,128)S(1)} custom-call(f32[1,128,128]{2,1,0:T(8,128)S(1)} %get-tuple-element.98), custom_call_target="InvertDiagBlocksLowerTriangular" | custom-call | tf_op jit(solution)/shard_map/jit(cholesky)/cholesky | solution.py:49
  123.7 1.7 convolution_subtract_fusion.2
  125.4 11.9 %cholesky.432 = f32[128,128]{1,0:T(8,128)S(1)} custom-call(f32[128,128]{1,0:T(8,128)S(1)} %cholesky.522), custom_call_target="Cholesky" | custom-call | tf_op jit(solution)/shard_map/jit(cholesky)/cholesky | solution.py:49
  137.3 9.8 %custom-call.59 = f32[1,128,128]{1,2,0:T(8,128)S(1)} custom-call(f32[1,128,128]{2,1,0:T(8,128)S(1)} %get-tuple-element.95), custom_call_target="InvertDiagBlocksLowerTriangular" | custom-call | tf_op jit(solution)/shard_map/jit(cholesky)/cholesky | solution.py:49
  147.4 1.7 convolution_subtract_fusion.3
  149.1 11.7 %cholesky.451 = f32[128,128]{1,0:T(8,128)S(1)} custom-call(f32[128,128]{1,0:T(8,128)S(1)} %cholesky.527), custom_call_target="Cholesky" | custom-call | tf_op jit(solution)/shard_map/jit(cholesky)/cholesky | solution.py:49
  160.9 9.8 %custom-call.60 = f32[1,128,128]{1,2,0:T(8,128)S(1)} custom-call(f32[1,128,128]{2,1,0:T(8,128)S(1)} %get-tuple-element.92), custom_call_target="InvertDiagBlocksLowerTriangular" | custom-call | tf_op jit(solution)/shard_map/jit(cholesky)/cholesky | solution.py:49
  170.9 1.5 convolution_subtract_fusion.4
  172.5 11.9 %cholesky.471 = f32[128,128]{1,0:T(8,128)S(1)} custom-call(f32[128,128]{1,0:T(8,128)S(1)} %cholesky.532), custom_call_target="Cholesky" | custom-call | tf_op jit(solution)/shard_map/jit(cholesky)/cholesky | solution.py:49
  184.4 9.8 %custom-call.61 = f32[1,128,128]{1,2,0:T(8,128)S(1)} custom-call(f32[1,128,128]{2,1,0:T(8,128)S(1)} %get-tuple-element.89), custom_call_target="InvertDiagBlocksLowerTriangular" | custom-call | tf_op jit(solution)/shard_map/jit(cholesky)/cholesky | solution.py:49
  194.4 1.2 convolution_subtract_fusion.5
  195.6 8.6 %cholesky.492 = f32[94,94]{1,0:T(8,128)S(1)} custom-call(f32[94,94]{1,0:T(8,128)S(1)} %convolution_subtract_fusion.5), custom_call_target="Cholesky" | custom-call | tf_op jit(solution)/shard_map/jit(cholesky)/cholesky | solution.py:49
  204.3 0.6 compare_reduce_fusion.4
  204.9 0.7 compare_reduce_fusion.3
  205.6 0.6 compare_reduce_fusion.2
  206.3 0.7 compare_reduce_fusion.1
  206.9 0.7 compare_reduce_fusion
  207.6 0.6 compare_reduce_fusion.5
  213.0 0.7 triangular_solve.510
  213.7 1.0 copy-done.1
  214.6 17.4 %while.4 = (s32[]{:T(128)}, f32[862,862]{1,0:T(8,128)}, s32[6,2]{0,1:T(2,128)S(1)}, f32[6,128,128]{2,1,0:T(8,128)S(1)}, s32[]{:T(128)}) while((s32[]{:T(128)}, f32[862,862]{1,0:T(8,128)}, s32[6,2]{0,1:T(2,128)S(1)}, f32[6,128,128]{2,1,0:T(8,128)S(1)}, s32[]{:T(128)}) %tuple.120), condition=%wide.while_cond.clone, body=%wide.while_body.clone.sunk | while | flops 2 | bytes 131189 | solution.py:25
  215.2 2.3 bitcast_dynamic-update-slice_fusion.2
  218.1 2.3 bitcast_dynamic-update-slice_fusion.2
  221.1 2.3 bitcast_dynamic-update-slice_fusion.2
  224.0 2.3 bitcast_dynamic-update-slice_fusion.2
  226.9 2.3 bitcast_dynamic-update-slice_fusion.2
  229.8 2.3 bitcast_dynamic-update-slice_fusion.2
  232.1 1.0 fusion.39
  233.1 0.8 pad_maximum_fusion
  234.0 69.8 %custom-call.64 = f32[7,128,128]{1,2,0:T(8,128)S(1)} custom-call(f32[7,128,128]{2,1,0:T(8,128)} %pad_maximum_fusion), custom_call_target="InvertDiagBlocksLowerTriangular" | custom-call | tf_op jit(solution)/shard_map/jit(_cho_solve)/triangular_solve | solution.py:25
  303.8 3.1 convolution_multiply_fusion
  313.2 0.8 convolution_dynamic-update-slice_fusion.6
  317.7 107.1 %all-reduce.7.cloned.1.call-done = f32[20,862]{1,0:T(8,128)} async-done(((f32[20,862]{1,0:T(8,128)}), f32[20,862]{1,0:T(8,128)}) %all-reduce.7.cloned.1.call-update) | async-done | bytes 68976 | tf_op jit(solution)/shard_map/psum | solution.py:29
  424.8 1.0 add_bitcast_fusion
  432.5 1.5 bitcast_add_fusion.1
  434.0 0.7 copy.13
  434.7 103.8 %all-reduce.9.cloned.1.call-done = f32[20,862]{1,0:T(8,128)} async-done(((f32[20,862]{1,0:T(8,128)}), f32[20,862]{1,0:T(8,128)}) %all-reduce.9.cloned.1.call-update) | async-done | bytes 68976 | tf_op jit(solution)/shard_map/psum | solution.py:29
  538.6 1.7 multiply_reduce_fusion.2
  540.3 0.9 subtract_bitcast_fusion
  541.2 0.7 copy.14
  541.9 40.7 %all-reduce.3 = (f32[1]{0:T(128)}, f32[1]{0:T(128)}, f32[1]{0:T(128)}, f32[1]{0:T(128)}) all-reduce(f32[1]{0:T(128)} %bitcast.80, f32[1]{0:T(128)} %bitcast.79, f32[1]{0:T(128)} %bitcast.77, f32[1]{0:T(128)} %bitcast.76), channel_id=1, replica_groups=mesh['slab'=16,'feat'=2] {'slab','feat'}, use_global_device_ids=true, to_apply=%region_23.25 | all-reduce | flops 4 | bytes 32 | tf_op jit(solution)/shard_map/psum | solution.py:61
  582.6 1.3 maximum_bitcast_fusion.1
  583.9 1.4 maximum_bitcast_fusion
  (183 shorter events, 29.9 us)
Async XLA Ops:
  7.2 11.2 %copy-start.10 = (f32[256]{0:T(256)S(1)}, f32[256]{0:T(256)}, u32[]{:S(2)}) copy-start(f32[256]{0:T(256)} %param.6) | copy-start | bytes 3076
  7.2 13.2 %copy-start.8 = (f32[40,256]{1,0:T(8,128)S(1)}, f32[40,256]{1,0:T(8,128)}, u32[]{:S(2)}) copy-start(f32[40,256]{1,0:T(8,128)} %param.7) | copy-start | bytes 122884
  7.2 417.6 %all-reduce.7.cloned.1.call-start = ((), (), s32[]{:S(2)}) async-start(), calls=%async_computation | async-start | bytes 172032 | tf_op jit(solution)/shard_map/psum | solution.py:29
  34.8 7.8 %copy-start = (f32[862,512]{1,0:T(8,128)}, f32[862,512]{1,0:T(8,128)S(1)}, u32[]{:S(2)}) copy-start(f32[862,512]{1,0:T(8,128)S(1)} %concatenate.45) | copy-start | bytes 5296132
  48.5 1.6 copy-start.3
  212.7 0.9 copy-start.9
  212.7 0.9 copy-start.11
  212.7 1.9 copy-start.6
  213.0 1.7 copy-start.1
  232.1 75.0 %copy-start.2 = (f32[862,862]{1,0:T(8,128)S(1)}, f32[862,862]{1,0:T(8,128)}, u32[]{:S(2)}) copy-start(f32[862,862]{1,0:T(8,128)} %get-tuple-element.201) | copy-start | bytes 8916532
  306.9 10.8 %copy-start.4 = (f32[20,862]{1,0:T(8,128)}, f32[20,862]{1,0:T(8,128)S(1)}, u32[]{:S(2)}) copy-start(f32[20,862]{1,0:T(8,128)S(1)} %convolution_multiply_fusion) | copy-start | bytes 206884
  317.7 220.9 %all-reduce.9.cloned.1.call-start = ((), (), s32[]{:S(2)}) async-start(), calls=%async_computation.1 | async-start | bytes 172032 | tf_op jit(solution)/shard_map/psum | solution.py:29
  424.8 7.6 %copy-start.5 = (f32[20,862]{1,0:T(8,128)S(1)}, f32[20,862]{1,0:T(8,128)}, u32[]{:S(2)}) copy-start(f32[20,862]{1,0:T(8,128)} %all-reduce.7.cloned.1.call-done) | copy-start | bytes 206884
  540.3 45.6 %copy-start.7 = (f32[20,862]{1,0:T(8,128)}, f32[20,862]{1,0:T(8,128)S(1)}, u32[]{:S(2)}) copy-start(f32[20,862]{1,0:T(8,128)S(1)} %get-tuple-element.45) | copy-start | bytes 206884
Sparse Core Ops, SparseCore 0:
  317.8 106.9 all-reduce.6
  434.1 104.3 all-reduce.8
where the time goes:
time: 600 us; the launch traced here: 593 us
  other arithmetic  236 us (39%)
  waiting for transfers between devices  211 us (35%)
  blocking collectives  46.8 us (8%)
  local copies, waits for them, and re-layouts  42.8 us (7%)
  matrix products  36.1 us (6%)
  between operations  20.1 us (3%)
    psum x2, waiting for transfers between devices, slab_average(): return lax.psum(summand, 'slab')  211 us
    another operation x26, other arithmetic, shards(): jnp.linalg.cholesky(gram_matrix + penalty * jnp.eye(width, dtype=jnp.floa...  145 us
    another operation x8, other arithmetic, solve_rows(): return jax.scipy.linalg.cho_solve((factor, True), right_side.T).T  73 us
    psum x1, blocking collectives, shards(): primal_sum, dual_sum = lax.psum((primal_part, dual_part), ('slab', 'feat'))  40.7 us
    another operation x26, local copies, waits for them, and re-layouts, solve_rows(): return jax.scipy.linalg.cho_solve((factor, True), right_side.T).T  18.6 us
    another operation x52, matrix products, solve_rows(): return jax.scipy.linalg.cho_solve((factor, True), right_side.T).T  13.1 us
    another operation x12, matrix products, shards(): jnp.linalg.cholesky(gram_matrix + penalty * jnp.eye(width, dtype=jnp.floa...  12.1 us
  transfers between devices with their start and end apart: 2, of which 2 were waited for; matrix products, arithmetic and copies ran while one was open for 0% of the time, Pallas kernels for 0%

commit v1 on v0

--- a/solution.py
+++ b/solution.py
@@ -26,7 +26,7 @@
 
 
 def slab_average(summand):
-    return lax.psum(summand, "slab")
+    return jnp.sum(lax.all_gather(summand, "slab"), axis=0)
 
 
 def shards(states, inputs, targets):

time: 600 us -> 505 us (0.84)
  waiting for transfers between devices: 211 us -> 115 us
    psum x2 -> x0, waiting for transfers between devices: 211 us -> none  [slab_average(): return lax.psum(summand, 'slab')]
    all_gather x0 -> x2, waiting for transfers between devices: none -> 115 us  [slab_average(): return jnp.sum(lax.all_gather(summand, 'slab'), axis=0)]
where the time goes in v1:
time: 505 us; the launch traced here: 498 us
  other arithmetic  240 us (48%)
  waiting for transfers between devices  115 us (23%)
  blocking collectives  44.7 us (9%)
  local copies, waits for them, and re-layouts  42.8 us (8%)
  matrix products  36.1 us (7%)
  between operations  20.1 us (4%)
    another operation x26, other arithmetic, shards(): jnp.linalg.cholesky(gram_matrix + penalty * jnp.eye(width, dtype=jnp.floa...  145 us
    all_gather x2, waiting for transfers between devices, slab_average(): return jnp.sum(lax.all_gather(summand, 'slab'), axis=0)  115 us
    another operation x8, other arithmetic, solve_rows(): return jax.scipy.linalg.cho_solve((factor, True), right_side.T).T  73 us
    psum x1, blocking collectives, shards(): primal_sum, dual_sum = lax.psum((primal_part, dual_part), ('slab', 'feat'))  38.6 us
    another operation x26, local copies, waits for them, and re-layouts, solve_rows(): return jax.scipy.linalg.cho_solve((factor, True), right_side.T).T  18.6 us
    another operation x52, matrix products, solve_rows(): return jax.scipy.linalg.cho_solve((factor, True), right_side.T).T  13.1 us
    another operation x12, matrix products, shards(): jnp.linalg.cholesky(gram_matrix + penalty * jnp.eye(width, dtype=jnp.floa...  12.1 us
    concatenate x1, local copies, waits for them, and re-layouts, features(): return jnp.concatenate(blocks, 0)  11.9 us
  transfers between devices with their start and end apart: 2, of which 2 were waited for; matrix products, arithmetic and copies ran while one was open for 0% of the time, Pallas kernels for 0%

profile of v1, /device:TPU:0, one launch (start us, length us, event | category | flops | bytes accessed | tf_op | source)
XLA Modules:
  0.0 498.4 jit_solution(4467598463079136576)
XLA Ops:
  7.2 2.2 all_gather.21
  9.5 0.6 slice_multiply_fusion.38
  18.4 1.9 all-gather.2
  20.3 2.0 all_gather.23
  22.9 11.9 %concatenate.45 = f32[862,512]{1,0:T(8,128)S(1)} concatenate(f32[40,512]{1,0:T(8,128)S(1)} %all_gather.21, f32[40,512]{1,0:T(8,128)S(1)} %broadcast_multiply_fusion.1, f32[39,512]{1,0:T(8,128)S(1)} %slice_multiply_fusion.6, f32[38,512]{1,0:T(8,128)S(1)} %slice_multiply_fusion.5, f32[37,512]{1,0:T(8,128)S(1)} %slice_multiply_fusion.4, f32[36,512]{1,0:T(8,128)S(1)} %slice_multiply_fusion.3, ...), dimensions={0} | concatenate | bytes 3530752 | tf_op jit(solution)/shard_map/concatenate | solution.py:17
  34.8 7.8 %convert_add_fusion = (f32[862,862]{0,1:T(8,128)}, f32[862,862]{0,1:T(8,128)}) fusion(f32[862,512]{1,0:T(8,128)S(1)} %concatenate.45), kind=kOutput, calls=%fused_computation.8 | convolution fusion | flops 4568234496 | bytes 7709728 | tf_op jit(solution)/shard_map/dot_general | solution.py:21
  42.6 3.6 copy.12
  46.3 2.3 fusion.1
  48.5 1.6 copy-done.3
  50.2 11.7 %cholesky.196 = f32[128,128]{1,0:T(8,128)S(1)} custom-call(f32[128,128]{1,0:T(8,128)S(1)} %cholesky.508), custom_call_target="Cholesky" | custom-call | tf_op jit(solution)/shard_map/jit(cholesky)/cholesky | solution.py:49
  62.1 9.8 %custom-call.56 = f32[1,128,128]{1,2,0:T(8,128)S(1)} custom-call(f32[1,128,128]{2,1,0:T(8,128)S(1)} %get-tuple-element.104), custom_call_target="InvertDiagBlocksLowerTriangular" | custom-call | tf_op jit(solution)/shard_map/jit(cholesky)/cholesky | solution.py:49
  72.0 1.4 constant_dynamic-update-slice_fusion.62
  73.4 1.5 convolution_subtract_fusion
  74.9 0.6 cholesky.512
  75.5 12.5 %cholesky.217 = f32[128,128]{1,0:T(8,128)S(1)} custom-call(f32[128,128]{1,0:T(8,128)} %cholesky.512), custom_call_target="Cholesky" | custom-call | tf_op jit(solution)/shard_map/jit(cholesky)/cholesky | solution.py:49
  88.1 0.6 select_reduce_fusion.4
  88.7 11.0 %custom-call.57 = f32[1,128,128]{1,2,0:T(8,128)S(1)} custom-call(f32[1,128,128]{2,1,0:T(8,128)} %get-tuple-element.101), custom_call_target="InvertDiagBlocksLowerTriangular" | custom-call | tf_op jit(solution)/shard_map/jit(cholesky)/cholesky | solution.py:49
  100.1 1.6 convolution_subtract_fusion.1
  101.8 11.7 %cholesky.413 = f32[128,128]{1,0:T(8,128)S(1)} custom-call(f32[128,128]{1,0:T(8,128)S(1)} %cholesky.517), custom_call_target="Cholesky" | custom-call | tf_op jit(solution)/shard_map/jit(cholesky)/cholesky | solution.py:49
  113.5 9.8 %custom-call.58 = f32[1,128,128]{1,2,0:T(8,128)S(1)} custom-call(f32[1,128,128]{2,1,0:T(8,128)S(1)} %get-tuple-element.98), custom_call_target="InvertDiagBlocksLowerTriangular" | custom-call | tf_op jit(solution)/shard_map/jit(cholesky)/cholesky | solution.py:49
  123.7 1.7 convolution_subtract_fusion.2
  125.4 11.9 %cholesky.432 = f32[128,128]{1,0:T(8,128)S(1)} custom-call(f32[128,128]{1,0:T(8,128)S(1)} %cholesky.522), custom_call_target="Cholesky" | custom-call | tf_op jit(solution)/shard_map/jit(cholesky)/cholesky | solution.py:49
  137.3 9.8 %custom-call.59 = f32[1,128,128]{1,2,0:T(8,128)S(1)} custom-call(f32[1,128,128]{2,1,0:T(8,128)S(1)} %get-tuple-element.95), custom_call_target="InvertDiagBlocksLowerTriangular" | custom-call | tf_op jit(solution)/shard_map/jit(cholesky)/cholesky | solution.py:49
  147.4 1.7 convolution_subtract_fusion.3
  149.1 11.7 %cholesky.451 = f32[128,128]{1,0:T(8,128)S(1)} custom-call(f32[128,128]{1,0:T(8,128)S(1)} %cholesky.527), custom_call_target="Cholesky" | custom-call | tf_op jit(solution)/shard_map/jit(cholesky)/cholesky | solution.py:49
  160.9 9.8 %custom-call.60 = f32[1,128,128]{1,2,0:T(8,128)S(1)} custom-call(f32[1,128,128]{2,1,0:T(8,128)S(1)} %get-tuple-element.92), custom_call_target="InvertDiagBlocksLowerTriangular" | custom-call | tf_op jit(solution)/shard_map/jit(cholesky)/cholesky | solution.py:49
  170.9 1.5 convolution_subtract_fusion.4
  172.5 11.9 %cholesky.471 = f32[128,128]{1,0:T(8,128)S(1)} custom-call(f32[128,128]{1,0:T(8,128)S(1)} %cholesky.532), custom_call_target="Cholesky" | custom-call | tf_op jit(solution)/shard_map/jit(cholesky)/cholesky | solution.py:49
  184.4 9.8 %custom-call.61 = f32[1,128,128]{1,2,0:T(8,128)S(1)} custom-call(f32[1,128,128]{2,1,0:T(8,128)S(1)} %get-tuple-element.89), custom_call_target="InvertDiagBlocksLowerTriangular" | custom-call | tf_op jit(solution)/shard_map/jit(cholesky)/cholesky | solution.py:49
  194.4 1.2 convolution_subtract_fusion.5
  195.6 8.6 %cholesky.492 = f32[94,94]{1,0:T(8,128)S(1)} custom-call(f32[94,94]{1,0:T(8,128)S(1)} %convolution_subtract_fusion.5), custom_call_target="Cholesky" | custom-call | tf_op jit(solution)/shard_map/jit(cholesky)/cholesky | solution.py:49
  204.3 0.6 compare_reduce_fusion.4
  204.9 0.7 compare_reduce_fusion.3
  205.6 0.6 compare_reduce_fusion.2
  206.3 0.7 compare_reduce_fusion.1
  206.9 0.7 compare_reduce_fusion
  207.6 0.6 compare_reduce_fusion.5
  213.0 0.7 triangular_solve.510
  213.7 1.0 copy-done.1
  214.6 17.4 %while.4 = (s32[]{:T(128)}, f32[862,862]{1,0:T(8,128)}, s32[6,2]{0,1:T(2,128)S(1)}, f32[6,128,128]{2,1,0:T(8,128)S(1)}, s32[]{:T(128)}) while((s32[]{:T(128)}, f32[862,862]{1,0:T(8,128)}, s32[6,2]{0,1:T(2,128)S(1)}, f32[6,128,128]{2,1,0:T(8,128)S(1)}, s32[]{:T(128)}) %tuple.120), condition=%wide.while_cond.clone, body=%wide.while_body.clone.sunk | while | flops 2 | bytes 131189 | solution.py:25
  215.2 2.3 bitcast_dynamic-update-slice_fusion.2
  218.1 2.3 bitcast_dynamic-update-slice_fusion.2
  221.1 2.3 bitcast_dynamic-update-slice_fusion.2
  224.0 2.3 bitcast_dynamic-update-slice_fusion.2
  226.9 2.3 bitcast_dynamic-update-slice_fusion.2
  229.8 2.3 bitcast_dynamic-update-slice_fusion.2
  232.1 1.0 fusion.40
  233.1 0.8 pad_maximum_fusion
  234.0 69.8 %custom-call.64 = f32[7,128,128]{1,2,0:T(8,128)S(1)} custom-call(f32[7,128,128]{2,1,0:T(8,128)} %pad_maximum_fusion), custom_call_target="InvertDiagBlocksLowerTriangular" | custom-call | tf_op jit(solution)/shard_map/jit(_cho_solve)/triangular_solve | solution.py:25
  303.8 3.1 convolution_multiply_fusion
  313.2 0.8 convolution_dynamic-update-slice_fusion.6
  317.7 59.6 %all-gather.8.cloned.1.call-done = f32[16,20,862]{2,1,0:T(8,128)} async-done(((f32[1,20,862]{2,1,0:T(8,128)}), f32[16,20,862]{2,1,0:T(8,128)}) %all-gather.8.cloned.1.call-update) | async-done | bytes 1103376 | tf_op jit(solution)/shard_map/all_gather | solution.py:29
  377.3 2.1 reduce_sum.54
  379.4 1.0 fusion.37
  387.0 1.5 fusion.108
  388.6 0.7 copy.13
  389.3 55.2 %all-gather.10.cloned.1.call-done = f32[16,20,862]{2,1,0:T(8,128)} async-done(((f32[1,20,862]{2,1,0:T(8,128)}), f32[16,20,862]{2,1,0:T(8,128)}) %all-gather.10.cloned.1.call-update) | async-done | bytes 1103376 | tf_op jit(solution)/shard_map/all_gather | solution.py:29
  444.5 1.4 reduce_sum.55
  445.9 1.7 multiply_reduce_fusion.2
  447.6 1.0 subtract_bitcast_fusion
  448.6 0.7 copy.14
  449.3 38.6 %all-reduce.3 = (f32[1]{0:T(128)}, f32[1]{0:T(128)}, f32[1]{0:T(128)}, f32[1]{0:T(128)}) all-reduce(f32[1]{0:T(128)} %bitcast.81, f32[1]{0:T(128)} %bitcast.80, f32[1]{0:T(128)} %bitcast.78, f32[1]{0:T(128)} %bitcast.77), channel_id=1, replica_groups=mesh['slab'=16,'feat'=2] {'slab','feat'}, use_global_device_ids=true, to_apply=%region_23.25 | all-reduce | flops 4 | bytes 32 | tf_op jit(solution)/shard_map/psum | solution.py:61
  487.8 1.3 maximum_bitcast_fusion.1
  489.2 1.3 maximum_bitcast_fusion
  (185 shorter events, 31.2 us)
Async XLA Ops:
  7.2 11.2 %copy-start.10 = (f32[256]{0:T(256)S(1)}, f32[256]{0:T(256)}, u32[]{:S(2)}) copy-start(f32[256]{0:T(256)} %param.6) | copy-start | bytes 3076
  7.2 13.2 %copy-start.8 = (f32[40,256]{1,0:T(8,128)S(1)}, f32[40,256]{1,0:T(8,128)}, u32[]{:S(2)}) copy-start(f32[40,256]{1,0:T(8,128)} %param.7) | copy-start | bytes 122884
  7.2 370.1 %all-gather.8.cloned.1.call-start = ((), (), s32[]{:S(2)}) async-start(), calls=%async_computation | async-start | bytes 1462272 | tf_op jit(solution)/shard_map/all_gather | solution.py:29
  34.8 7.8 %copy-start = (f32[862,512]{1,0:T(8,128)}, f32[862,512]{1,0:T(8,128)S(1)}, u32[]{:S(2)}) copy-start(f32[862,512]{1,0:T(8,128)S(1)} %concatenate.45) | copy-start | bytes 5296132
  48.5 1.6 copy-start.3
  212.7 0.9 copy-start.9
  212.7 0.9 copy-start.11
  212.7 1.9 copy-start.6
  213.0 1.7 copy-start.1
  232.1 75.0 %copy-start.2 = (f32[862,862]{1,0:T(8,128)S(1)}, f32[862,862]{1,0:T(8,128)}, u32[]{:S(2)}) copy-start(f32[862,862]{1,0:T(8,128)} %get-tuple-element.201) | copy-start | bytes 8916532
  306.9 10.8 %copy-start.5 = (f32[862,20]{0,1:T(8,128)}, f32[862,20]{0,1:T(8,128)S(1)}, u32[]{:S(2)}) copy-start(f32[862,20]{0,1:T(8,128)S(1)} %convolution_multiply_fusion) | copy-start | bytes 206884
  317.7 126.8 %all-gather.10.cloned.1.call-start = ((), (), s32[]{:S(2)}) async-start(), calls=%async_computation.1 | async-start | bytes 1462272 | tf_op jit(solution)/shard_map/all_gather | solution.py:29
  379.3 7.6 %copy-start.4 = (f32[20,862]{1,0:T(8,128)S(1)}, f32[20,862]{1,0:T(8,128)}, u32[]{:S(2)}) copy-start(f32[20,862]{1,0:T(8,128)} %reduce_sum.54) | copy-start | bytes 206884
  447.6 43.5 %copy-start.7 = (f32[20,862]{1,0:T(8,128)}, f32[20,862]{1,0:T(8,128)S(1)}, u32[]{:S(2)}) copy-start(f32[20,862]{1,0:T(8,128)S(1)} %get-tuple-element.45) | copy-start | bytes 206884
Sparse Core Ops, SparseCore 0:
  317.8 59.4 all-gather.7
  388.7 55.7 all-gather.9
